TPU v7x, 32 devices: a whole 2x2x4 slice. The times are simulated.
32 devices in a mesh: fsdp: 8 (over z, y), seq: 4 (over x, core).
Axes of the slice: x: 2, y: 2, z: 4, core: 2. Of those that a mesh axis runs over, the one named last changes fastest.
Arguments:
- tokens: bfloat16 [8, 1024, 768], P('fsdp', 'seq'), may hold values from -6 to 6
- condition: bfloat16 [8, 768], P('fsdp'), may hold values from -6 to 6
- ada_weight: bfloat16 [2, 768, 4608], P(None, 'fsdp'), may hold values from -0.21875 to 0.21875
- ada_bias: bfloat16 [2, 4608], P(None, 'fsdp'), may hold values from -3 to 3
- qkv_weight: bfloat16 [2, 768, 2304], P(None, 'fsdp'), may hold values from -0.21875 to 0.21875
- qv_bias: bfloat16 [2, 1536], P(None, 'fsdp'), may hold values from -3 to 3
- out_weight: bfloat16 [2, 768, 768], P(None, 'fsdp'), may hold values from -1.25 to 1.25
- out_bias: bfloat16 [2, 768], P(None, 'fsdp'), may hold values from -3 to 3
- up_weight: bfloat16 [2, 768, 3072], P(None, 'fsdp'), may hold values from -0.21875 to 0.21875
- up_bias: bfloat16 [2, 3072], P(None, 'fsdp'), may hold values from -3 to 3
- down_weight: bfloat16 [2, 3072, 768], P(None, 'fsdp'), may hold values from -0.109375 to 0.109375
- down_bias: bfloat16 [2, 768], P(None, 'fsdp'), may hold values from -3 to 3
- cotangent: bfloat16 [8, 1024, 768], P('fsdp', 'seq'), may hold values from -6 to 6
Outputs:
- block_out: bfloat16 [8, 1024, 768], P('fsdp', 'seq')
- grad_tokens: float32 [8, 1024, 768], P('fsdp', 'seq')
- grad_condition: float32 [8, 768], P('fsdp')
- grad_ada_weight: float32 [2, 768, 4608], P(None, 'fsdp')
- grad_ada_bias: float32 [2, 4608], P(None, 'fsdp')
- grad_qkv_weight: float32 [2, 768, 2304], P(None, 'fsdp')
- grad_qv_bias: float32 [2, 1536], P(None, 'fsdp')
- grad_out_weight: float32 [2, 768, 768], P(None, 'fsdp')
- grad_out_bias: float32 [2, 768], P(None, 'fsdp')
- grad_up_weight: float32 [2, 768, 3072], P(None, 'fsdp')
- grad_up_bias: float32 [2, 3072], P(None, 'fsdp')
- grad_down_weight: float32 [2, 3072, 768], P(None, 'fsdp')
- grad_down_bias: float32 [2, 768], P(None, 'fsdp')
All inputs are finite; a program needn't handle non-finite values.
Results may differ from a plain program's by a relative error of at most 0.017.
The roundings to bfloat16 on the way count: a program that leaves them out, or rounds other values in their place, can miss the bound.
Values may be sent and summed in bfloat16 or wider, within the bound.
A program may use at most 256 MiB of HBM per device.

v0:
```python
import jax
import jax.numpy as jnp
from jax import lax
from jax.sharding import PartitionSpec as P

HEAD_DIM = 64
SCORE_SCALE = HEAD_DIM ** (-0.5)
EPSILON = 1e-06
HIGHEST = lax.Precision.HIGHEST
F32 = jnp.float32
BF16 = jnp.bfloat16


def normalize(values):
    centred = values - jnp.mean(values, axis=-1, keepdims=True)
    inverse = lax.rsqrt(jnp.mean(centred * centred, axis=-1, keepdims=True) + EPSILON)
    return (centred * inverse, inverse)


def norm_back(gradient, normed, inverse):
    return inverse * (
        gradient
        - jnp.mean(gradient, axis=-1, keepdims=True)
        - normed * jnp.mean(gradient * normed, axis=-1, keepdims=True)
    )


def mm(a, b):
    return lax.dot_general(a, b, (((1,), (0,)), ((), ())), preferred_element_type=F32)


def mm_nt(a, b):
    return lax.dot_general(a, b, (((1,), (1,)), ((), ())), preferred_element_type=F32)


def mm_tn(a, b):
    return lax.dot_general(a, b, (((0,), (0,)), ((), ())), preferred_element_type=F32)


def split_heads(rows):
    return rows.reshape(rows.shape[0], -1, HEAD_DIM).transpose(1, 0, 2)


def join_heads(heads):
    return heads.transpose(1, 0, 2).reshape(heads.shape[1], -1)


def attend(q, k, v):
    q, k, v = (split_heads(q), split_heads(k), split_heads(v))
    scores = jnp.einsum("hqd,hkd->hqk", q, k, preferred_element_type=F32) * SCORE_SCALE
    logsum = jnp.log(jnp.sum(jnp.exp(scores), axis=-1, keepdims=True))
    prob = jnp.exp(scores - logsum).astype(BF16)
    out = jnp.einsum("hqk,hkd->hqd", prob, v, preferred_element_type=F32)
    return (join_heads(out).astype(BF16), logsum)


def attend_back(q, k, v, logsum, out_grad):
    q, k, v, out_grad = (split_heads(q), split_heads(k), split_heads(v), split_heads(out_grad))
    scores = jnp.einsum("hqd,hkd->hqk", q, k, preferred_element_type=F32) * SCORE_SCALE
    prob = jnp.exp(scores - logsum)
    dv = jnp.einsum("hqk,hqd->hkd", prob.astype(BF16), out_grad, preferred_element_type=F32)
    dp = jnp.einsum("hqd,hkd->hqk", out_grad, v, preferred_element_type=F32)
    inner = jnp.sum(prob * dp, axis=-1, keepdims=True)
    ds = (prob * (dp - inner)).astype(BF16)
    dq = jnp.einsum("hqk,hkd->hqd", ds, k, preferred_element_type=F32) * SCORE_SCALE
    dk = jnp.einsum("hqk,hqd->hkd", ds, q, preferred_element_type=F32) * SCORE_SCALE
    return [join_heads(t).astype(BF16) for t in (dq, dk, dv)]


def gelu_parts(u):
    c = 0.7978845608028654
    inner = c * (u + 0.044715 * (u * u * u))
    t = jnp.tanh(inner)
    value = 0.5 * u * (1.0 + t)
    slope = 0.5 * (1.0 + t) + 0.5 * u * (1.0 - t * t) * (c * (1.0 + 3.0 * 0.044715 * u * u))
    return (value, slope)


def per_device(
    tokens,
    condition,
    ada_weight,
    ada_bias,
    qkv_weight,
    qv_bias,
    out_weight,
    out_bias,
    up_weight,
    up_bias,
    down_weight,
    down_bias,
    cotangent,
):
    n = lax.axis_size("fsdp")
    ns = lax.axis_size("seq")
    f = lax.axis_index("fsdp")
    s = lax.axis_index("seq")
    layers, rows, width6 = ada_weight.shape
    width = rows * n
    ff = up_weight.shape[2]
    hc = width // ns
    fc = ff // (ns * n)

    def take(x, axis):
        return lax.dynamic_index_in_dim(x, s, axis, keepdims=False)

    def own(x, axis, size):
        return lax.dynamic_slice_in_dim(x, f * size, size, axis)

    w_qkv, w_rest = ([], [])
    for l in range(layers):
        q_part = take(qkv_weight[l].reshape(rows, 3, ns, hc), 2).reshape(rows, 3 * hc)
        u_part = take(up_weight[l].reshape(rows, n, ns, fc), 2).reshape(rows, n * fc)
        d_part = take(down_weight[l].reshape(ns, fc, width), 0)
        w_qkv.append(lax.all_gather(q_part, "fsdp", axis=0, tiled=True))
        rest = jnp.concatenate([u_part, d_part, out_weight[l]], axis=1)
        w_rest.append(lax.all_gather(rest, "fsdp", axis=0, tiled=True))
    fw = n * fc
    cond_float = condition.astype(F32)
    cond_act = jax.nn.silu(cond_float).astype(BF16)
    small = jnp.concatenate(
        [
            ada_bias.reshape(-1),
            qv_bias.reshape(-1),
            out_bias.reshape(-1),
            up_bias.reshape(-1),
            down_bias.reshape(-1),
            cond_act.reshape(-1),
        ]
    )
    small = lax.all_gather(small, "fsdp", axis=0, tiled=False)
    pos = 0

    def unpack(per_layer):
        nonlocal pos
        part = small[:, pos : pos + layers * per_layer].reshape(n, layers, per_layer)
        pos += layers * per_layer
        return part.transpose(1, 0, 2).reshape(layers, n * per_layer)

    ada_b = unpack(ada_bias.shape[1]).astype(F32)
    qv_b = unpack(qv_bias.shape[1]).astype(F32)
    out_b = unpack(out_bias.shape[1]).astype(F32)
    up_b = unpack(up_bias.shape[1]).astype(F32)
    down_b = unpack(down_bias.shape[1]).astype(F32)
    cond_all = small[:, pos:]
    cond_rows = own(cond_all, 1, rows)
    q_b = take(qv_b[:, :width].reshape(layers, ns, hc), 1)
    v_b = take(qv_b[:, width:].reshape(layers, ns, hc), 1)
    qkv_b = jnp.concatenate([q_b, jnp.zeros_like(q_b), v_b], axis=1)
    up_bs = take(up_b.reshape(layers, n, ns, fc), 2).reshape(layers, fw)
    mod_partial = jnp.stack([mm(cond_rows, ada_weight[l]) for l in range(layers)], axis=1)
    mod = lax.psum_scatter(mod_partial, "fsdp", scatter_dimension=0, tiled=True)[0] + ada_b
    hidden = tokens[0].astype(F32)
    saved = []
    for l in range(layers):
        shift_a, scale_a, gate_a, shift_m, scale_m, gate_m = jnp.split(mod[l], 6)
        n_a, r_a = normalize(hidden)
        attn_in = (n_a * (1.0 + scale_a) + shift_a).astype(BF16)
        attn_all = lax.all_gather(attn_in, "seq", axis=0, tiled=True)
        qkv = (mm(attn_all, w_qkv[l]) + qkv_b[l]).astype(BF16)
        q, k, v = (qkv[:, :hc], qkv[:, hc : 2 * hc], qkv[:, 2 * hc :])
        head_out, logsum = attend(q, k, v)
        tok_out = lax.all_to_all(head_out, "seq", split_axis=0, concat_axis=1, tiled=True)
        branch = mm(tok_out, w_rest[l][:, fw + width :]) + out_b[l]
        middle = hidden + gate_a * branch
        n_m, r_m = normalize(middle)
        mlp_in = (n_m * (1.0 + scale_m) + shift_m).astype(BF16)
        mlp_all = lax.all_gather(mlp_in, "seq", axis=0, tiled=True)
        up = mm(mlp_all, w_rest[l][:, :fw]) + up_bs[l]
        act = gelu_parts(up)[0].astype(BF16)
        feed = mm(act, w_rest[l][:, fw : fw + width])
        feed = lax.psum_scatter(feed, "seq", scatter_dimension=0, tiled=True) + down_b[l]
        saved.append(
            (n_a, r_a, attn_all, q, k, v, logsum, tok_out, branch, n_m, r_m, mlp_all, up, act, feed)
        )
        hidden = middle + gate_m * feed
    block_out = hidden.astype(BF16)
    g = cotangent[0].astype(F32)
    d_mods = [None] * layers
    reduced = [None] * layers
    bias_grads = [None] * layers
    for l in reversed(range(layers)):
        shift_a, scale_a, gate_a, shift_m, scale_m, gate_m = jnp.split(mod[l], 6)
        n_a, r_a, attn_all, q, k, v, logsum, tok_out, branch, n_m, r_m, mlp_all, up, act, feed = (
            saved[l]
        )
        g_feed = (gate_m * g).astype(BF16)
        d_gate_m = jnp.sum(g * feed, axis=0)
        g_feed_all = lax.all_gather(g_feed, "seq", axis=0, tiled=True)
        grad_down = mm_tn(act, g_feed_all)
        g_up = (mm_nt(g_feed_all, w_rest[l][:, fw : fw + width]) * gelu_parts(up)[1]).astype(BF16)
        grad_up = mm_tn(mlp_all, g_up)
        g_min = lax.psum_scatter(
            mm_nt(g_up, w_rest[l][:, :fw]), "seq", scatter_dimension=0, tiled=True
        )
        d_scale_m = jnp.sum(g_min * n_m, axis=0)
        d_shift_m = jnp.sum(g_min, axis=0)
        g_mid = g + norm_back(g_min * (1.0 + scale_m), n_m, r_m)
        g_branch = (gate_a * g_mid).astype(BF16)
        d_gate_a = jnp.sum(g_mid * branch, axis=0)
        grad_out = mm_tn(tok_out, g_branch)
        g_o = mm_nt(g_branch, w_rest[l][:, fw + width :]).astype(BF16)
        g_o_heads = lax.all_to_all(g_o, "seq", split_axis=1, concat_axis=0, tiled=True)
        dq, dk, dv = attend_back(q, k, v, logsum, g_o_heads)
        g_qkv = jnp.concatenate([dq, dk, dv], axis=1)
        grad_qkv = mm_tn(attn_all, g_qkv)
        g_ain = lax.psum_scatter(mm_nt(g_qkv, w_qkv[l]), "seq", scatter_dimension=0, tiled=True)
        d_scale_a = jnp.sum(g_ain * n_a, axis=0)
        d_shift_a = jnp.sum(g_ain, axis=0)
        g = g_mid + norm_back(g_ain * (1.0 + scale_a), n_a, r_a)
        d_mods[l] = jnp.concatenate(
            [d_shift_a, d_scale_a, d_gate_a, d_shift_m, d_scale_m, d_gate_m]
        )
        packed = jnp.concatenate([grad_up, grad_down, grad_out, grad_qkv], axis=1).astype(BF16)
        reduced[l] = lax.psum_scatter(packed, "fsdp", scatter_dimension=0, tiled=True)

        def place(x, axis):
            zeros = jnp.zeros(x.shape[:axis] + (ns,) + x.shape[axis + 1 :], F32)
            return lax.dynamic_update_slice_in_dim(zeros, x, s, axis)

        qv_g = place(
            jnp.stack([jnp.sum(dq.astype(F32), axis=0), jnp.sum(dv.astype(F32), axis=0)])[
                :, None, :
            ],
            1,
        )
        up_g = place(jnp.sum(g_up.astype(F32), axis=0).reshape(n, 1, fc), 1)
        bias_grads[l] = jnp.concatenate(
            [
                qv_g.reshape(n, -1),
                jnp.sum(g_branch.astype(F32), axis=0).reshape(n, -1),
                up_g.reshape(n, -1),
                jnp.sum(g_feed.astype(F32), axis=0).reshape(n, -1),
            ],
            axis=1,
        )
    red = jnp.stack(reduced)
    shared = jnp.concatenate([red[:, :, : fw + width], red[:, :, fw + 2 * width :]], axis=2)
    shared = lax.all_gather(shared, "seq", axis=0, tiled=False).astype(F32)
    grad_up = (
        shared[..., :fw]
        .reshape(ns, layers, rows, n, fc)
        .transpose(1, 2, 3, 0, 4)
        .reshape(layers, rows, ff)
    )
    grad_down = shared[..., fw : fw + width].transpose(1, 0, 2, 3).reshape(layers, ns * fc, width)
    grad_qkv = shared[..., fw + width :].reshape(ns, layers, rows, 3, hc).transpose(1, 2, 3, 0, 4)
    grad_qkv = grad_qkv.reshape(layers, rows, 3 * width)
    grad_out = lax.psum(red[:, :, fw + width : fw + 2 * width], "seq").astype(F32)
    bias = lax.psum(jnp.stack(bias_grads), ("fsdp", "seq"))
    bias = lax.dynamic_index_in_dim(bias, f, 1, keepdims=False)
    cuts = [qv_bias.shape[1], out_bias.shape[1], up_bias.shape[1], down_bias.shape[1]]
    grad_bias, at = ([], 0)
    for size in cuts:
        grad_bias.append(bias[:, at : at + size])
        at += size
    d_mod = lax.psum(jnp.stack(d_mods), "seq")
    d_mod_all = lax.all_gather(d_mod, "fsdp", axis=0, tiled=False)
    cond_rows32 = cond_rows.astype(F32)
    grad_ada = jnp.stack(
        [
            lax.dot_general(
                cond_rows32,
                d_mod_all[:, l],
                (((0,), (0,)), ((), ())),
                precision=HIGHEST,
                preferred_element_type=F32,
            )
            for l in range(layers)
        ]
    )
    grad_ada_bias = own(jnp.sum(d_mod_all, axis=0), 1, width6 // n)
    g_cond = sum(
        (
            lax.dot_general(
                d_mod_all[:, l],
                ada_weight[l].astype(F32),
                (((1,), (1,)), ((), ())),
                precision=HIGHEST,
                preferred_element_type=F32,
            )
            for l in range(layers)
        )
    )
    g_cond = lax.all_to_all(g_cond, "fsdp", split_axis=0, concat_axis=1, tiled=True)
    _, silu_back = jax.vjp(jax.nn.silu, cond_float)
    grad_condition = silu_back(g_cond)[0]
    return (
        block_out[None],
        g[None],
        grad_condition,
        grad_ada,
        grad_ada_bias,
        grad_qkv,
        grad_bias[0],
        grad_out,
        grad_bias[1],
        grad_up,
        grad_bias[2],
        grad_down,
        grad_bias[3],
    )


def solution(mesh):
    token = P("fsdp", "seq", None)
    matrix = P(None, "fsdp", None)
    vector = P(None, "fsdp")
    return jax.shard_map(
        per_device,
        mesh=mesh,
        in_specs=(token, P("fsdp", None)) + (matrix, vector) * 5 + (token,),
        out_specs=(token, token, P("fsdp", None)) + (matrix, vector) * 5,
        check_vma=False,
    )
```

profile of v0, /device:TPU:0, one launch (start us, length us, event | category | flops | bytes accessed | tf_op | source)
XLA Modules:
  0.0 1008.6 jit_solution(16156190823706369313)
XLA Ops:
  12.4 32.4 %all-gather.2 = bf16[8,1,3456]{2,1,0:T(2,128)(2,1)S(1)} all-gather(bf16[1,1,3456]{2,1,0:T(2,128)(2,1)S(1)} %reshape.391), channel_id=2, replica_groups=mesh['fsdp'=8,'seq'=4] {'fsdp'}, dimensions={0}, use_global_device_ids=true | all-gather | bytes 62208 | tf_op jit(solution)/shard_map/all_gather | solution.py:131
  50.2 71.0 %all-reduce.6.cloned.1.call-done = f32[8,2,4608]{2,1,0:T(2,128)} async-done(((f32[8,2,4608]{2,1,0:T(2,128)}), f32[8,2,4608]{2,1,0:T(2,128)}) %all-reduce.6.cloned.1.call-update) | async-done | bytes 294928
  135.6 34.4 %all_gather.51 = bf16[768,576]{1,0:T(8,128)(2,1)S(1)} all-gather(bf16[96,576]{1,0:T(8,128)(2,1)S(1)} %copy.123), channel_id=1, replica_groups=mesh['fsdp'=8,'seq'=4] {'fsdp'}, dimensions={0}, use_global_device_ids=true | all-gather | bytes 995328 | tf_op jit(solution)/shard_map/all_gather | solution.py:115
  197.6 14.9 %all-gather.15.cloned.1.call-done = bf16[768,2304]{1,0:T(8,128)(2,1)} async-done(((bf16[96,2304]{1,0:T(8,128)(2,1)}), bf16[768,2304]{1,0:T(8,128)(2,1)}) %all-gather.15.cloned.1.call-update) | async-done | bytes 3538960 | tf_op jit(solution)/shard_map/all_gather | solution.py:117
  216.7 18.2 %all-gather.17.cloned.1.call-done = bf16[1024,768]{1,0:T(8,128)(2,1)} async-done(((bf16[256,768]{1,0:T(8,128)(2,1)}), bf16[1024,768]{1,0:T(8,128)(2,1)}) %all-gather.17.cloned.1.call-update) | async-done | bytes 1572880 | tf_op jit(solution)/shard_map/all_gather | solution.py:168
  244.9 37.9 %reduce-scatter.13.cloned.1.call-done = f32[256,768]{1,0:T(8,128)} async-done(((f32[1024,768]{1,0:T(8,128)}), f32[256,768]{1,0:T(8,128)}) %reduce-scatter.13.cloned.1.call-update) | async-done | bytes 786448 | tf_op jit(solution)/shard_map/reduce_scatter | solution.py:172
  289.8 32.9 %all_gather.55 = bf16[768,576]{1,0:T(8,128)(2,1)S(1)} all-gather(bf16[96,576]{1,0:T(8,128)(2,1)S(1)} %copy.129), channel_id=1, replica_groups=mesh['fsdp'=8,'seq'=4] {'fsdp'}, dimensions={0}, use_global_device_ids=true | all-gather | bytes 995328 | tf_op jit(solution)/shard_map/all_gather | solution.py:115
  343.8 28.8 %all-gather.21.cloned.1.call-done = bf16[768,2304]{1,0:T(8,128)(2,1)} async-done(((bf16[96,2304]{1,0:T(8,128)(2,1)}), bf16[768,2304]{1,0:T(8,128)(2,1)}) %all-gather.21.cloned.1.call-update) | async-done | bytes 3538960 | tf_op jit(solution)/shard_map/all_gather | solution.py:117
  377.7 17.5 %all-gather.23.cloned.1.call-done = bf16[1024,768]{1,0:T(8,128)(2,1)} async-done(((bf16[256,768]{1,0:T(8,128)(2,1)}), bf16[1024,768]{1,0:T(8,128)(2,1)}) %all-gather.23.cloned.1.call-update) | async-done | bytes 1572880 | tf_op jit(solution)/shard_map/all_gather | solution.py:168
  400.0 17.0 %all-gather.25.cloned.1.call-done = bf16[1024,768]{1,0:T(8,128)(2,1)} async-done(((bf16[256,768]{1,0:T(8,128)(2,1)}), bf16[1024,768]{1,0:T(8,128)(2,1)}) %all-gather.25.cloned.1.call-update) | async-done | bytes 1572880 | tf_op jit(solution)/shard_map/all_gather | solution.py:189
  434.2 31.9 %reduce-scatter.17.cloned.1.call-done = f32[256,768]{1,0:T(8,128)} async-done(((f32[1024,768]{1,0:T(8,128)}), f32[256,768]{1,0:T(8,128)}) %reduce-scatter.17.cloned.1.call-update) | async-done | bytes 786448 | tf_op jit(solution)/shard_map/reduce_scatter | solution.py:193
  467.6 38.9 %reduce-scatter.15.cloned.1.call-done = f32[256,768]{1,0:T(8,128)} async-done(((f32[1024,768]{1,0:T(8,128)}), f32[256,768]{1,0:T(8,128)}) %reduce-scatter.15.cloned.1.call-update) | async-done | bytes 786448 | tf_op jit(solution)/shard_map/reduce_scatter | solution.py:172
  511.5 10.2 %all_to_all.80 = bf16[256,4,192]{0,2,1:T(8,128)(2,1)S(1)} all-to-all(bf16[256,4,192]{0,2,1:T(8,128)(2,1)S(1)} %bitcast.284), channel_id=1, replica_groups=mesh['fsdp'=8,'seq'=4] {'seq'}, dimensions={1} | all-to-all | bytes 786432 | tf_op jit(solution)/shard_map/all_to_all | solution.py:203
  553.4 38.0 %reduce-scatter.19.cloned.1.call-done = f32[256,768]{1,0:T(8,128)} async-done(((f32[1024,768]{1,0:T(8,128)}), f32[256,768]{1,0:T(8,128)}) %reduce-scatter.19.cloned.1.call-update) | async-done | bytes 786448 | tf_op jit(solution)/shard_map/reduce_scatter | solution.py:207
  595.5 19.6 %all-gather.27.cloned.1.call-done = bf16[1024,768]{1,0:T(8,128)(2,1)} async-done(((bf16[256,768]{1,0:T(8,128)(2,1)}), bf16[1024,768]{1,0:T(8,128)(2,1)}) %all-gather.27.cloned.1.call-update) | async-done | bytes 1572880 | tf_op jit(solution)/shard_map/all_gather | solution.py:189
  643.2 21.0 %reduce-scatter.21.cloned.1.call-done = f32[256,768]{1,0:T(8,128)} async-done(((f32[1024,768]{1,0:T(8,128)}), f32[256,768]{1,0:T(8,128)}) %reduce-scatter.21.cloned.1.call-update) | async-done | bytes 786448 | tf_op jit(solution)/shard_map/reduce_scatter | solution.py:193
  670.2 10.0 all_to_all.81
  680.8 11.1 %multiply_reduce_fusion = (f32[3,1024]{1,0:T(4,128)S(1)}, f32[3,1024,1024]{1,2,0:T(8,128)}) fusion(f32[3,1024,1024]{1,2,0:T(8,128)} %fusion.3, bf16[3,1024,64]{1,2,0:T(8,128)(2,1)S(1)} %bitcast.272, bf16[1024,3,64]{0,2,1:T(8,128)(2,1)S(1)} %reshape.363), kind=kOutput, calls=%fused_computation.7 | convolution fusion | flops 408941568 | bytes 25964544 | tf_op jit(solution)/shard_map/hqd,hkd->hqk/dot_general | solution.py:62
  691.9 10.3 %multiply_convert_fusion = bf16[3,1024,1024]{1,2,0:T(8,128)(2,1)S(1)} fusion(f32[3,1024,1024]{1,2,0:T(8,128)} %fusion.3, f32[3,1024,1024]{1,2,0:T(8,128)} %get-tuple-element.173, f32[3,1024]{1,0:T(4,128)S(1)} %get-tuple-element.172), kind=kLoop, calls=%fused_computation.6 | loop fusion | flops 9437184 | bytes 31469568 | tf_op jit(solution)/shard_map/convert_element_type | solution.py:64
  728.6 32.6 %reduce-scatter.27.cloned.1.call-done = bf16[96,2880]{1,0:T(8,128)(2,1)} async-done(((bf16[768,2880]{1,0:T(8,128)(2,1)}), bf16[96,2880]{1,0:T(8,128)(2,1)}) %reduce-scatter.27.cloned.1.call-update) | async-done | bytes 552976
  763.2 40.9 %psum.22 = f32[2,8,768]{2,0,1:T(2,128)S(1)} all-reduce(f32[2,8,768]{2,0,1:T(2,128)S(1)} %pad_maximum_fusion.14), channel_id=1, replica_groups=mesh['fsdp'=8,'seq'=4] {'fsdp','seq'}, use_global_device_ids=true, to_apply=%region_53.54 | all-reduce | flops 12288 | bytes 98304 | tf_op jit(solution)/shard_map/psum | solution.py:250
  807.6 92.1 %reduce-scatter.25.cloned.1.call-done = bf16[96,2880]{1,0:T(8,128)(2,1)} async-done(((bf16[768,2880]{1,0:T(8,128)(2,1)}), bf16[96,2880]{1,0:T(8,128)(2,1)}) %reduce-scatter.25.cloned.1.call-update) | async-done | bytes 552976
  908.4 11.1 %psum.21 = f32[1,2,4608]{2,1,0:T(2,128)S(1)} all-reduce(f32[1,2,4608]{2,1,0:T(2,128)S(1)} %maximum_bitcast_fusion), channel_id=1, replica_groups=mesh['fsdp'=8,'seq'=4] {'seq'}, use_global_device_ids=true, to_apply=%region_39.40 | all-reduce | flops 9216 | bytes 73728 | tf_op jit(solution)/shard_map/psum | solution.py:257
  919.5 31.0 %all_gather.61 = f32[8,2,4608]{2,1,0:T(2,128)S(1)} all-gather(f32[1,2,4608]{2,1,0:T(2,128)S(1)} %psum.21), channel_id=1, replica_groups=mesh['fsdp'=8,'seq'=4] {'fsdp'}, dimensions={0}, use_global_device_ids=true | all-gather | bytes 331776 | tf_op jit(solution)/shard_map/all_gather | solution.py:258
  (423 shorter events, 289.5 us)
Async XLA Ops:
  7.2 113.9 %all-reduce.6.cloned.1.call-start = ((), (), s32[]{:S(2)}) async-start(), calls=%async_computation.31 | async-start | bytes 589824
  44.8 79.0 %copy-start.29 = (bf16[2,96,3072]{2,1,0:T(8,128)(2,1)S(1)}, bf16[2,96,3072]{2,1,0:T(8,128)(2,1)}, u32[]{:S(2)}) copy-start(bf16[2,96,3072]{2,1,0:T(8,128)(2,1)} %param.21) | copy-start | bytes 3538948
  48.8 121.1 %all-gather.13.cloned.1.call-start = ((), (), s32[]{:S(2)}) async-start(), calls=%async_computation.13 | async-start | bytes 1966080 | tf_op jit(solution)/shard_map/all_gather | solution.py:159
  123.7 88.8 %all-gather.15.cloned.1.call-start = ((), (), s32[]{:S(2)}) async-start(), calls=%async_computation.14 | async-start | bytes 3981312 | tf_op jit(solution)/shard_map/all_gather | solution.py:117
  186.8 10.8 %all-to-all-start = ((bf16[4,256,192]{1,2,0:T(8,128)(2,1)}), bf16[4,256,192]{1,2,0:T(8,128)(2,1)S(1)}, u32[]{:S(2)}, u32[]{:S(2)}) async-start(bf16[4,256,192]{1,2,0:T(8,128)(2,1)} %copy.126), calls=%async_computation | async-start | bytes 786432 | tf_op jit(solution)/shard_map/all_to_all | solution.py:163
  190.2 44.7 %all-gather.17.cloned.1.call-start = ((), (), s32[]{:S(2)}) async-start(), calls=%async_computation.15 | async-start | bytes 1966080 | tf_op jit(solution)/shard_map/all_gather | solution.py:168
  216.4 66.4 %reduce-scatter.13.cloned.1.call-start = ((), (), s32[]{:S(2)}) async-start(), calls=%async_computation.16 | async-start | bytes 3932160 | tf_op jit(solution)/shard_map/reduce_scatter | solution.py:172
  244.8 77.9 %all-gather.19.cloned.1.call-start = ((), (), s32[]{:S(2)}) async-start(), calls=%async_computation.17 | async-start | bytes 1966080 | tf_op jit(solution)/shard_map/all_gather | solution.py:159
  285.4 87.2 %all-gather.21.cloned.1.call-start = ((), (), s32[]{:S(2)}) async-start(), calls=%async_computation.18 | async-start | bytes 3981312 | tf_op jit(solution)/shard_map/all_gather | solution.py:117
  340.0 32.6 %all-to-all-start.1 = ((bf16[4,256,192]{1,2,0:T(8,128)(2,1)}), bf16[4,256,192]{1,2,0:T(8,128)(2,1)S(1)}, u32[]{:S(2)}, u32[]{:S(2)}) async-start(bf16[4,256,192]{1,2,0:T(8,128)(2,1)} %copy.131), calls=%async_computation.2 | async-start | bytes 786432 | tf_op jit(solution)/shard_map/all_to_all | solution.py:163
  343.5 51.7 %all-gather.23.cloned.1.call-start = ((), (), s32[]{:S(2)}) async-start(), calls=%async_computation.19 | async-start | bytes 1966080 | tf_op jit(solution)/shard_map/all_gather | solution.py:168
  376.7 40.3 %all-gather.25.cloned.1.call-start = ((), (), s32[]{:S(2)}) async-start(), calls=%async_computation.21 | async-start | bytes 1966080 | tf_op jit(solution)/shard_map/all_gather | solution.py:189
  377.6 88.5 %reduce-scatter.17.cloned.1.call-start = ((), (), s32[]{:S(2)}) async-start(), calls=%async_computation.22 | async-start | bytes 3932160 | tf_op jit(solution)/shard_map/reduce_scatter | solution.py:193
  428.0 78.5 %reduce-scatter.15.cloned.1.call-start = ((), (), s32[]{:S(2)}) async-start(), calls=%async_computation.20 | async-start | bytes 3932160 | tf_op jit(solution)/shard_map/reduce_scatter | solution.py:172
  434.1 157.3 %reduce-scatter.19.cloned.1.call-start = ((), (), s32[]{:S(2)}) async-start(), calls=%async_computation.23 | async-start | bytes 3932160 | tf_op jit(solution)/shard_map/reduce_scatter | solution.py:207
  553.4 61.7 %all-gather.27.cloned.1.call-start = ((), (), s32[]{:S(2)}) async-start(), calls=%async_computation.24 | async-start | bytes 1966080 | tf_op jit(solution)/shard_map/all_gather | solution.py:189
  595.3 68.9 %reduce-scatter.21.cloned.1.call-start = ((), (), s32[]{:S(2)}) async-start(), calls=%async_computation.25 | async-start | bytes 3932160 | tf_op jit(solution)/shard_map/reduce_scatter | solution.py:193
  626.2 135.1 %reduce-scatter.27.cloned.1.call-start = ((), (), s32[]{:S(2)}) async-start(), calls=%async_computation.30 | async-start | bytes 5087232
  643.2 162.8 %reduce-scatter.23.cloned.1.call-start = ((), (), s32[]{:S(2)}) async-start(), calls=%async_computation.26 | async-start | bytes 3932160 | tf_op jit(solution)/shard_map/reduce_scatter | solution.py:207
  710.9 188.8 %reduce-scatter.25.cloned.1.call-start = ((), (), s32[]{:S(2)}) async-start(), calls=%async_computation.29 | async-start | bytes 5087232
  727.4 78.6 %copy-start.48 = (f32[256]{0:T(256)S(1)}, f32[256]{0:T(256)}, u32[]{:S(2)}) copy-start(f32[256]{0:T(256)} %copy-done.47) | copy-start | bytes 3076
  727.4 239.0 %all-reduce.4.cloned.1.call-start = ((), (), s32[]{:S(2)}) async-start(), calls=%async_computation.27 | async-start | bytes 786432 | tf_op jit(solution)/shard_map/psum | solution.py:249
  902.9 65.5 %all-gather.29.cloned.1.call-start = ((), (), s32[]{:S(2)}) async-start(), calls=%async_computation.28 | async-start | bytes 4177920 | tf_op jit(solution)/shard_map/all_gather | solution.py:239
  953.1 11.6 %all-to-all-start.4 = ((f32[8,1,96]{2,1,0:T(1,128)}), f32[8,1,96]{2,1,0:T(1,128)S(1)}, u32[]{:S(2)}, u32[]{:S(2)}) async-start(f32[8,1,96]{2,1,0:T(1,128)} %bitcast.68), calls=%async_computation.10 | async-start | bytes 8192 | tf_op jit(solution)/shard_map/all_to_all | solution.py:285
  (66 other events, 1097.1 us)
Sparse Core Ops, SparseCore 0:
  49.0 72.1 all-reduce.5
  123.8 18.6 all-gather.12
  145.3 67.1 all-gather.14
  216.5 18.3 all-gather.16
  244.9 37.8 reduce-scatter.12
  285.5 19.6 all-gather.18
  307.9 64.5 all-gather.20
  376.8 18.3 all-gather.22
  397.3 19.6 all-gather.24
  428.2 37.8 reduce-scatter.16
  468.6 37.8 reduce-scatter.14
  553.5 37.8 reduce-scatter.18
  595.4 19.6 all-gather.26
  626.3 37.8 reduce-scatter.20
  667.7 93.5 reduce-scatter.26
  764.2 37.6 reduce-scatter.22
  805.4 94.2 reduce-scatter.24
  903.1 32.5 all-reduce.3
  937.8 29.6 all-gather.28
where the time goes:
time: 1020 us; the launch traced here: 1010 us
  waiting for transfers between devices  487 us (48%)
  blocking collectives  203 us (20%)
  matrix products  144 us (14%)
  local copies, waits for them, and re-layouts  90.3 us (9%)
  other arithmetic  55.2 us (5%)
  between operations  15.6 us (2%)
  starting transfers between devices  13.8 us (1%)
    unnamed x22, waiting for transfers between devices  196 us
    reduce_scatter x2, waiting for transfers between devices, per_device(): lax.psum_scatter(feed, 'seq', scatter_dimension=0, tiled=True) + down_b[l]  76.8 us
    all_gather x2, blocking collectives, per_device(): w_qkv.append(lax.all_gather(q_part, 'fsdp', axis=0, tiled=True))  67.3 us
    reduce_scatter x2, waiting for transfers between devices, per_device(): lax.psum_scatter(mm_nt(g_up, w_rest[l][:, :fw]), 'seq', scatter_dimension...  52.9 us
    all_gather x2, waiting for transfers between devices, per_device(): w_rest.append(lax.all_gather(rest, 'fsdp', axis=0, tiled=True))  43.6 us
    psum x1, blocking collectives, per_device(): bias = lax.psum(jnp.stack(bias_grads), ('fsdp', 'seq'))  40.9 us
    reduce_scatter x2, waiting for transfers between devices, per_device(): lax.psum_scatter(mm_nt(g_qkv, w_qkv[l]), 'seq', scatter_dimension=0, tile...  38 us
    all_gather x2, waiting for transfers between devices, per_device(): g_feed_all = lax.all_gather(g_feed, 'seq', axis=0, tiled=True)  36.6 us
  transfers between devices with their start and end apart: 22, of which 16 were waited for; matrix products, arithmetic and copies ran while one was open for 15% of the time, Pallas kernels for 0%

commit v1 on v0

--- a/solution.py
+++ b/solution.py
@@ -9,6 +9,22 @@
 HIGHEST = lax.Precision.HIGHEST
 F32 = jnp.float32
 BF16 = jnp.bfloat16
+
+
+def pairwise_exchange(shard, axis, split, join):
+    ways, here = (lax.axis_size(axis), lax.axis_index(axis))
+    width = shard.shape[split] // ways
+    shape = list(shard.shape)
+    shape[split] = width
+    height = shape[join]
+    shape[join] = height * ways
+    full = jnp.zeros(shape, shard.dtype)
+    for mask in range(ways):
+        part = lax.dynamic_slice_in_dim(shard, (here ^ mask) * width, width, axis=split)
+        if mask:
+            part = lax.ppermute(part, axis, [(d, d ^ mask) for d in range(ways)])
+        full = lax.dynamic_update_slice_in_dim(full, part, (here ^ mask) * height, axis=join)
+    return full
 
 
 def normalize(values):
@@ -200,7 +216,7 @@
         d_gate_a = jnp.sum(g_mid * branch, axis=0)
         grad_out = mm_tn(tok_out, g_branch)
         g_o = mm_nt(g_branch, w_rest[l][:, fw + width :]).astype(BF16)
-        g_o_heads = lax.all_to_all(g_o, "seq", split_axis=1, concat_axis=0, tiled=True)
+        g_o_heads = pairwise_exchange(g_o, "seq", 1, 0)
         dq, dk, dv = attend_back(q, k, v, logsum, g_o_heads)
         g_qkv = jnp.concatenate([dq, dk, dv], axis=1)
         grad_qkv = mm_tn(attn_all, g_qkv)

time: 1020 us -> 1020 us (level)
  blocking collectives: 203 us -> 183 us
  waiting for transfers between devices: 487 us -> 503 us
    all_to_all x2 -> x0, blocking collectives: 20.2 us -> none  [per_device(): lax.all_to_all(g_o, 'seq', split_axis=1, concat_axis=0, tiled=True)]
    ppermute x0 -> x6, waiting for transfers between devices: none -> 13.1 us  [pairwise_exchange(): part = lax.ppermute(part, axis, [(d, d ^ mask) for d in range(ways)])]
  transfers between devices with their start and end apart: 22 -> 28, of which waited for: 16 -> 18; matrix products, arithmetic and copies ran while one was open for 15% -> 15% of each run, Pallas kernels for 0% -> 0%
where the time goes in v1:
time: 1020 us; the launch traced here: 1010 us
  waiting for transfers between devices  503 us (49%)
  blocking collectives  183 us (18%)
  matrix products  145 us (14%)
  local copies, waits for them, and re-layouts  90.7 us (9%)
  other arithmetic  51.7 us (5%)
  starting transfers between devices  18.9 us (2%)
  between operations  15.7 us (2%)
    unnamed x22, waiting for transfers between devices  200 us
    reduce_scatter x2, waiting for transfers between devices, per_device(): lax.psum_scatter(feed, 'seq', scatter_dimension=0, tiled=True) + down_b[l]  76.8 us
    all_gather x2, blocking collectives, per_device(): w_qkv.append(lax.all_gather(q_part, 'fsdp', axis=0, tiled=True))  67.3 us
    reduce_scatter x2, waiting for transfers between devices, per_device(): lax.psum_scatter(mm_nt(g_up, w_rest[l][:, :fw]), 'seq', scatter_dimension...  52.2 us
    all_gather x2, waiting for transfers between devices, per_device(): w_rest.append(lax.all_gather(rest, 'fsdp', axis=0, tiled=True))  43.6 us
    psum x1, blocking collectives, per_device(): bias = lax.psum(jnp.stack(bias_grads), ('fsdp', 'seq'))  40.9 us
    reduce_scatter x2, waiting for transfers between devices, per_device(): lax.psum_scatter(mm_nt(g_qkv, w_qkv[l]), 'seq', scatter_dimension=0, tile...  38 us
    all_gather x2, waiting for transfers between devices, per_device(): g_feed_all = lax.all_gather(g_feed, 'seq', axis=0, tiled=True)  36.6 us
  transfers between devices with their start and end apart: 28, of which 18 were waited for; matrix products, arithmetic and copies ran while one was open for 15% of the time, Pallas kernels for 0%

profile of v1, /device:TPU:0, one launch (start us, length us, event | category | flops | bytes accessed | tf_op | source)
XLA Modules:
  0.0 1007.7 jit_solution(6210588304399299064)
XLA Ops:
  12.4 32.4 %all-gather.2 = bf16[8,1,3456]{2,1,0:T(2,128)(2,1)S(1)} all-gather(bf16[1,1,3456]{2,1,0:T(2,128)(2,1)S(1)} %reshape.383), channel_id=2, replica_groups=mesh['fsdp'=8,'seq'=4] {'fsdp'}, dimensions={0}, use_global_device_ids=true | all-gather | bytes 62208 | tf_op jit(solution)/shard_map/all_gather | solution.py:147
  50.2 71.0 %all-reduce.6.cloned.1.call-done = f32[8,2,4608]{2,1,0:T(2,128)} async-done(((f32[8,2,4608]{2,1,0:T(2,128)}), f32[8,2,4608]{2,1,0:T(2,128)}) %all-reduce.6.cloned.1.call-update) | async-done | bytes 294928
  135.6 34.4 %all_gather.51 = bf16[768,576]{1,0:T(8,128)(2,1)S(1)} all-gather(bf16[96,576]{1,0:T(8,128)(2,1)S(1)} %copy.121), channel_id=1, replica_groups=mesh['fsdp'=8,'seq'=4] {'fsdp'}, dimensions={0}, use_global_device_ids=true | all-gather | bytes 995328 | tf_op jit(solution)/shard_map/all_gather | solution.py:131
  173.0 6.9 fusion.3
  197.6 14.9 %all-gather.15.cloned.1.call-done = bf16[768,2304]{1,0:T(8,128)(2,1)} async-done(((bf16[96,2304]{1,0:T(8,128)(2,1)}), bf16[768,2304]{1,0:T(8,128)(2,1)}) %all-gather.15.cloned.1.call-update) | async-done | bytes 3538960 | tf_op jit(solution)/shard_map/all_gather | solution.py:133
  216.7 18.2 %all-gather.17.cloned.1.call-done = bf16[1024,768]{1,0:T(8,128)(2,1)} async-done(((bf16[256,768]{1,0:T(8,128)(2,1)}), bf16[1024,768]{1,0:T(8,128)(2,1)}) %all-gather.17.cloned.1.call-update) | async-done | bytes 1572880 | tf_op jit(solution)/shard_map/all_gather | solution.py:184
  244.9 37.9 %reduce-scatter.13.cloned.1.call-done = f32[256,768]{1,0:T(8,128)} async-done(((f32[1024,768]{1,0:T(8,128)}), f32[256,768]{1,0:T(8,128)}) %reduce-scatter.13.cloned.1.call-update) | async-done | bytes 786448 | tf_op jit(solution)/shard_map/reduce_scatter | solution.py:188
  289.8 32.9 %all_gather.55 = bf16[768,576]{1,0:T(8,128)(2,1)S(1)} all-gather(bf16[96,576]{1,0:T(8,128)(2,1)S(1)} %copy.127), channel_id=1, replica_groups=mesh['fsdp'=8,'seq'=4] {'fsdp'}, dimensions={0}, use_global_device_ids=true | all-gather | bytes 995328 | tf_op jit(solution)/shard_map/all_gather | solution.py:131
  326.3 6.9 fusion.2
  343.8 28.8 %all-gather.21.cloned.1.call-done = bf16[768,2304]{1,0:T(8,128)(2,1)} async-done(((bf16[96,2304]{1,0:T(8,128)(2,1)}), bf16[768,2304]{1,0:T(8,128)(2,1)}) %all-gather.21.cloned.1.call-update) | async-done | bytes 3538960 | tf_op jit(solution)/shard_map/all_gather | solution.py:133
  377.7 17.5 %all-gather.23.cloned.1.call-done = bf16[1024,768]{1,0:T(8,128)(2,1)} async-done(((bf16[256,768]{1,0:T(8,128)(2,1)}), bf16[1024,768]{1,0:T(8,128)(2,1)}) %all-gather.23.cloned.1.call-update) | async-done | bytes 1572880 | tf_op jit(solution)/shard_map/all_gather | solution.py:184
  400.0 17.0 %all-gather.25.cloned.1.call-done = bf16[1024,768]{1,0:T(8,128)(2,1)} async-done(((bf16[256,768]{1,0:T(8,128)(2,1)}), bf16[1024,768]{1,0:T(8,128)(2,1)}) %all-gather.25.cloned.1.call-update) | async-done | bytes 1572880 | tf_op jit(solution)/shard_map/all_gather | solution.py:205
  434.7 31.4 %reduce-scatter.17.cloned.1.call-done = f32[256,768]{1,0:T(8,128)} async-done(((f32[1024,768]{1,0:T(8,128)}), f32[256,768]{1,0:T(8,128)}) %reduce-scatter.17.cloned.1.call-update) | async-done | bytes 786448 | tf_op jit(solution)/shard_map/reduce_scatter | solution.py:209
  467.6 38.9 %reduce-scatter.15.cloned.1.call-done = f32[256,768]{1,0:T(8,128)} async-done(((f32[1024,768]{1,0:T(8,128)}), f32[256,768]{1,0:T(8,128)}) %reduce-scatter.15.cloned.1.call-update) | async-done | bytes 786448 | tf_op jit(solution)/shard_map/reduce_scatter | solution.py:188
  522.2 7.5 convert_reduce_fusion.5
  552.5 38.0 %reduce-scatter.19.cloned.1.call-done = f32[256,768]{1,0:T(8,128)} async-done(((f32[1024,768]{1,0:T(8,128)}), f32[256,768]{1,0:T(8,128)}) %reduce-scatter.19.cloned.1.call-update) | async-done | bytes 786448 | tf_op jit(solution)/shard_map/reduce_scatter | solution.py:223
  594.6 19.6 %all-gather.27.cloned.1.call-done = bf16[1024,768]{1,0:T(8,128)(2,1)} async-done(((bf16[256,768]{1,0:T(8,128)(2,1)}), bf16[1024,768]{1,0:T(8,128)(2,1)}) %all-gather.27.cloned.1.call-update) | async-done | bytes 1572880 | tf_op jit(solution)/shard_map/all_gather | solution.py:205
  642.5 20.8 %reduce-scatter.21.cloned.1.call-done = f32[256,768]{1,0:T(8,128)} async-done(((f32[1024,768]{1,0:T(8,128)}), f32[256,768]{1,0:T(8,128)}) %reduce-scatter.21.cloned.1.call-update) | async-done | bytes 786448 | tf_op jit(solution)/shard_map/reduce_scatter | solution.py:209
  678.4 11.7 %multiply_reduce_fusion = (f32[3,1024]{1,0:T(4,128)S(1)}, f32[3,1024,1024]{1,2,0:T(8,128)}) fusion(f32[3,1024,1024]{1,2,0:T(8,128)} %fusion.3, bf16[3,1024,64]{1,2,0:T(8,128)(2,1)S(1)} %bitcast.259, bf16[3,1024,64]{1,2,0:T(8,128)(2,1)S(1)} %bitcast.256), kind=kOutput, calls=%fused_computation.7 | convolution fusion | flops 408941568 | bytes 25964544 | tf_op jit(solution)/shard_map/hqd,hkd->hqk/dot_general | solution.py:78
  723.4 36.9 %reduce-scatter.27.cloned.1.call-done = bf16[96,2880]{1,0:T(8,128)(2,1)} async-done(((bf16[768,2880]{1,0:T(8,128)(2,1)}), bf16[96,2880]{1,0:T(8,128)(2,1)}) %reduce-scatter.27.cloned.1.call-update) | async-done | bytes 552976
  762.2 40.9 %psum.22 = f32[2,8,768]{2,0,1:T(2,128)S(1)} all-reduce(f32[2,8,768]{2,0,1:T(2,128)S(1)} %pad_maximum_fusion.14), channel_id=1, replica_groups=mesh['fsdp'=8,'seq'=4] {'fsdp','seq'}, use_global_device_ids=true, to_apply=%region_53.54 | all-reduce | flops 12288 | bytes 98304 | tf_op jit(solution)/shard_map/psum | solution.py:266
  806.7 92.1 %reduce-scatter.25.cloned.1.call-done = bf16[96,2880]{1,0:T(8,128)(2,1)} async-done(((bf16[768,2880]{1,0:T(8,128)(2,1)}), bf16[96,2880]{1,0:T(8,128)(2,1)}) %reduce-scatter.25.cloned.1.call-update) | async-done | bytes 552976
  907.5 11.0 %psum.21 = f32[1,2,4608]{2,1,0:T(2,128)S(1)} all-reduce(f32[1,2,4608]{2,1,0:T(2,128)S(1)} %maximum_bitcast_fusion), channel_id=1, replica_groups=mesh['fsdp'=8,'seq'=4] {'seq'}, use_global_device_ids=true, to_apply=%region_39.40 | all-reduce | flops 9216 | bytes 73728 | tf_op jit(solution)/shard_map/psum | solution.py:273
  918.6 31.0 %all_gather.61 = f32[8,2,4608]{2,1,0:T(2,128)S(1)} all-gather(f32[1,2,4608]{2,1,0:T(2,128)S(1)} %psum.21), channel_id=1, replica_groups=mesh['fsdp'=8,'seq'=4] {'fsdp'}, dimensions={0}, use_global_device_ids=true | all-gather | bytes 331776 | tf_op jit(solution)/shard_map/all_gather | solution.py:274
  (440 shorter events, 293.4 us)
Async XLA Ops:
  7.2 113.9 %all-reduce.6.cloned.1.call-start = ((), (), s32[]{:S(2)}) async-start(), calls=%async_computation.29 | async-start | bytes 589824
  48.8 121.1 %all-gather.13.cloned.1.call-start = ((), (), s32[]{:S(2)}) async-start(), calls=%async_computation.11 | async-start | bytes 1966080 | tf_op jit(solution)/shard_map/all_gather | solution.py:175
  123.7 88.8 %all-gather.15.cloned.1.call-start = ((), (), s32[]{:S(2)}) async-start(), calls=%async_computation.12 | async-start | bytes 3981312 | tf_op jit(solution)/shard_map/all_gather | solution.py:133
  186.8 10.8 %all-to-all-start = ((bf16[4,256,192]{1,2,0:T(8,128)(2,1)}), bf16[4,256,192]{1,2,0:T(8,128)(2,1)S(1)}, u32[]{:S(2)}, u32[]{:S(2)}) async-start(bf16[4,256,192]{1,2,0:T(8,128)(2,1)} %copy.124), calls=%async_computation | async-start | bytes 786432 | tf_op jit(solution)/shard_map/all_to_all | solution.py:179
  190.2 44.7 %all-gather.17.cloned.1.call-start = ((), (), s32[]{:S(2)}) async-start(), calls=%async_computation.13 | async-start | bytes 1966080 | tf_op jit(solution)/shard_map/all_gather | solution.py:184
  216.4 66.4 %reduce-scatter.13.cloned.1.call-start = ((), (), s32[]{:S(2)}) async-start(), calls=%async_computation.14 | async-start | bytes 3932160 | tf_op jit(solution)/shard_map/reduce_scatter | solution.py:188
  244.8 77.9 %all-gather.19.cloned.1.call-start = ((), (), s32[]{:S(2)}) async-start(), calls=%async_computation.15 | async-start | bytes 1966080 | tf_op jit(solution)/shard_map/all_gather | solution.py:175
  285.4 87.2 %all-gather.21.cloned.1.call-start = ((), (), s32[]{:S(2)}) async-start(), calls=%async_computation.16 | async-start | bytes 3981312 | tf_op jit(solution)/shard_map/all_gather | solution.py:133
  340.0 32.6 %all-to-all-start.1 = ((bf16[4,256,192]{1,2,0:T(8,128)(2,1)}), bf16[4,256,192]{1,2,0:T(8,128)(2,1)S(1)}, u32[]{:S(2)}, u32[]{:S(2)}) async-start(bf16[4,256,192]{1,2,0:T(8,128)(2,1)} %copy.129), calls=%async_computation.2 | async-start | bytes 786432 | tf_op jit(solution)/shard_map/all_to_all | solution.py:179
  343.5 51.7 %all-gather.23.cloned.1.call-start = ((), (), s32[]{:S(2)}) async-start(), calls=%async_computation.17 | async-start | bytes 1966080 | tf_op jit(solution)/shard_map/all_gather | solution.py:184
  376.7 40.3 %all-gather.25.cloned.1.call-start = ((), (), s32[]{:S(2)}) async-start(), calls=%async_computation.19 | async-start | bytes 1966080 | tf_op jit(solution)/shard_map/all_gather | solution.py:205
  377.6 88.5 %reduce-scatter.17.cloned.1.call-start = ((), (), s32[]{:S(2)}) async-start(), calls=%async_computation.20 | async-start | bytes 3932160 | tf_op jit(solution)/shard_map/reduce_scatter | solution.py:209
  428.0 78.5 %reduce-scatter.15.cloned.1.call-start = ((), (), s32[]{:S(2)}) async-start(), calls=%async_computation.18 | async-start | bytes 3932160 | tf_op jit(solution)/shard_map/reduce_scatter | solution.py:188
  434.1 156.4 %reduce-scatter.19.cloned.1.call-start = ((), (), s32[]{:S(2)}) async-start(), calls=%async_computation.21 | async-start | bytes 3932160 | tf_op jit(solution)/shard_map/reduce_scatter | solution.py:223
  512.4 8.9 collective-permute-start.2
  552.4 61.7 %all-gather.27.cloned.1.call-start = ((), (), s32[]{:S(2)}) async-start(), calls=%async_computation.22 | async-start | bytes 1966080 | tf_op jit(solution)/shard_map/all_gather | solution.py:205
  594.4 68.9 %reduce-scatter.21.cloned.1.call-start = ((), (), s32[]{:S(2)}) async-start(), calls=%async_computation.23 | async-start | bytes 3932160 | tf_op jit(solution)/shard_map/reduce_scatter | solution.py:209
  625.2 135.1 %reduce-scatter.27.cloned.1.call-start = ((), (), s32[]{:S(2)}) async-start(), calls=%async_computation.28 | async-start | bytes 5087232
  642.2 162.8 %reduce-scatter.23.cloned.1.call-start = ((), (), s32[]{:S(2)}) async-start(), calls=%async_computation.24 | async-start | bytes 3932160 | tf_op jit(solution)/shard_map/reduce_scatter | solution.py:223
  669.5 8.7 collective-permute-start.5
  705.7 193.0 %reduce-scatter.25.cloned.1.call-start = ((), (), s32[]{:S(2)}) async-start(), calls=%async_computation.27 | async-start | bytes 5087232
  722.2 243.3 %all-reduce.4.cloned.1.call-start = ((), (), s32[]{:S(2)}) async-start(), calls=%async_computation.25 | async-start | bytes 786432 | tf_op jit(solution)/shard_map/psum | solution.py:265
  902.0 65.5 %all-gather.29.cloned.1.call-start = ((), (), s32[]{:S(2)}) async-start(), calls=%async_computation.26 | async-start | bytes 4177920 | tf_op jit(solution)/shard_map/all_gather | solution.py:255
  952.1 11.6 %all-to-all-start.2 = ((f32[8,1,96]{2,1,0:T(1,128)}), f32[8,1,96]{2,1,0:T(1,128)S(1)}, u32[]{:S(2)}, u32[]{:S(2)}) async-start(f32[8,1,96]{2,1,0:T(1,128)} %bitcast.68), calls=%async_computation.8 | async-start | bytes 8192 | tf_op jit(solution)/shard_map/all_to_all | solution.py:301
  (72 other events, 1248.2 us)
Sparse Core Ops, SparseCore 0:
  49.0 72.1 all-reduce.5
  123.8 18.6 all-gather.12
  145.3 67.1 all-gather.14
  216.5 18.3 all-gather.16
  244.9 37.8 reduce-scatter.12
  285.5 19.6 all-gather.18
  307.9 64.5 all-gather.20
  376.8 18.3 all-gather.22
  397.3 19.6 all-gather.24
  428.2 37.8 reduce-scatter.16
  468.6 37.8 reduce-scatter.14
  552.6 37.8 reduce-scatter.18
  594.5 19.6 all-gather.26
  625.3 37.8 reduce-scatter.20
  666.7 93.5 reduce-scatter.26
  763.3 37.6 reduce-scatter.22
  804.5 94.2 reduce-scatter.24
  902.1 32.6 all-reduce.3
  936.9 29.6 all-gather.28
